TPU v7x, 32 devices: a whole 2x2x4 slice. The times are simulated.
32 devices in a mesh: replica: 16 (over z, x, core), spatial: 2 (over y).
Axes of the slice: x: 2, y: 2, z: 4, core: 2. Of those that a mesh axis runs over, the one named last changes fastest.
Arguments:
- grads: bfloat16 [16, 2, 852992], P('replica', 'spatial'), may hold values from -6 to 6
- master: float32 [852992], P(('replica', 'spatial')), may hold values from -0.06 to 0.06
- velocity: float32 [852992], P(('replica', 'spatial')), may hold values from -0.3 to 0.3
- layer_offsets: int32 [6], replicated, may hold values from 0 to 852736, as said below
- layer_sizes: int32 [6], replicated, may hold values from 256 to 589824
- lars_skip: int32 [6], replicated, may hold values from 0 to 1
Outputs:
- new_weights: bfloat16 [852992], replicated
- new_master: float32 [852992], P(('replica', 'spatial'))
- new_velocity: float32 [852992], P(('replica', 'spatial'))
Inputs may be any that keep to these rules, and one draw needn't show every extreme that they name: layer_offsets, layer_sizes and lars_skip describe the six tensors (a 256 x 1024 convolution, a 256 x 256 x 9 convolution, and two gains and two shifts of 256 entries) laid end to end in some order without gaps, the last of them always a gain or a shift; lars_skip is 1 exactly for the gains and shifts.
All inputs are finite; a program needn't handle non-finite values.
Results may differ from a plain program's by a relative error of at most 0.001.
Values may be sent and summed in bfloat16 or wider, within the bound.
A program may use at most 64 MiB of HBM per device.

v0:
```python
import jax
import jax.numpy as jnp
from jax import lax
from jax.sharding import PartitionSpec as P


def shards(grads, master, velocity, layer_offsets, layer_sizes, lars_skip):
    n_rep = lax.axis_size("replica")
    n_spa = lax.axis_size("spatial")
    shard = master.shape[0]
    position = lax.axis_index(("replica", "spatial")) * shard + jnp.arange(shard, dtype=jnp.int32)
    inside = (position[None, :] >= layer_offsets[:, None]) & (
        position[None, :] < (layer_offsets + layer_sizes)[:, None]
    )
    onehot = inside.astype(jnp.float32)
    received = lax.all_to_all(
        grads[0, 0].reshape(n_rep, n_spa * shard),
        "replica",
        split_axis=0,
        concat_axis=0,
        tiled=True,
    )
    first = jnp.sum(received.astype(jnp.float32), axis=0)
    summed = lax.psum_scatter(
        first.reshape(n_spa, shard), "spatial", scatter_dimension=0, tiled=True
    )
    grad = summed.reshape(shard) / (n_rep * n_spa)
    gsq_local = jnp.dot(onehot, grad * grad, precision=lax.Precision.HIGHEST)
    wsq_local = jnp.dot(onehot, master * master, precision=lax.Precision.HIGHEST)
    wsq, gsq = lax.psum((wsq_local, gsq_local), ("replica", "spatial"))
    wnorm = jnp.sqrt(wsq)
    gnorm = jnp.sqrt(gsq)
    skipped = lars_skip.astype(jnp.float32)
    ratio = 0.02 * wnorm / (gnorm + 0.001 * wnorm + 1e-06)
    trust = skipped + (1.0 - skipped) * ratio
    decay = (1.0 - skipped) * 0.001
    trust_pos = jnp.dot(trust, onehot, precision=lax.Precision.HIGHEST)
    decay_pos = jnp.dot(decay, onehot, precision=lax.Precision.HIGHEST)
    new_velocity = 0.9 * velocity + 8.0 * trust_pos * (grad + decay_pos * master)
    new_master = master - new_velocity
    new_weights = lax.all_gather(
        new_master.astype(jnp.bfloat16), ("replica", "spatial"), axis=0, tiled=True
    )
    return (new_weights, new_master, new_velocity)


def solution(mesh):
    return jax.shard_map(
        shards,
        mesh=mesh,
        in_specs=(
            P("replica", "spatial", None),
            P(("replica", "spatial")),
            P(("replica", "spatial")),
            P(),
            P(),
            P(),
        ),
        out_specs=(P(), P(("replica", "spatial")), P(("replica", "spatial"))),
        check_vma=False,
    )
```

profile of v0, /device:TPU:0, one launch (start us, length us, event | category | flops | bytes accessed | tf_op | source)
XLA Modules:
  0.0 341.0 jit_solution(4959349934665128111)
XLA Ops:
  7.2 37.8 %reduce.1 = bf16[852992]{0:T(1024)(128)(2,1)} reduce(bf16[1,1,852992]{2,1,0:T(2,128)(2,1)} %param.6, bf16[]{:T(256)} %constant.38), dimensions={0,1}, to_apply=%param.6.reduce_sub_computation | reduce | bytes 3411970 | tf_op args[0]
  44.9 3.0 all_to_all.8
  47.9 0.5 broadcast.54
  48.4 13.3 %reduce.8 = bf16[16,53312]{1,0:T(8,128)(2,1)} reduce(bf16[16,1,53312]{2,1,0:T(2,128)(2,1)S(1)} %all_to_all.8, bf16[]{:T(256)} %broadcast.54), dimensions={1}, to_apply=%all_to_all.8.reduce_sub_computation | reduce | bytes 3411970 | tf_op jit(solution)/shard_map/all_to_all | solution.py:16
  61.8 3.2 reshape.38
  65.0 0.0 copy-start.1
  65.0 0.0 copy-start.4
  65.0 0.0 copy-start.6
  65.0 0.0 copy-start.7
  65.0 7.6 %all-to-all-start = ((bf16[16,2,26656]{2,1,0:T(2,128)(2,1)}), bf16[16,2,26656]{2,1,0:T(2,128)(2,1)}, u32[]{:S(2)}, u32[]{:S(2)}) async-start(bf16[16,2,26656]{2,1,0:T(2,128)(2,1)} %reshape.38), calls=%async_computation | async-start | bytes 3424256 | tf_op jit(solution)/shard_map/all_to_all | solution.py:16
  72.5 0.0 all-reduce.8.cloned.1.call-start
  72.6 0.0 copy-done.1
  72.6 0.7 reshape.25
  73.4 0.0 copy-done.4
  73.4 0.0 copy-done.6
  73.4 0.0 copy-done.7
  73.4 0.7 dynamic-slice
  74.1 0.7 iota_add_fusion
  74.7 32.2 %all-to-all-done = bf16[16,2,26656]{2,1,0:T(2,128)(2,1)} async-done(((bf16[16,2,26656]{2,1,0:T(2,128)(2,1)}), bf16[16,2,26656]{2,1,0:T(2,128)(2,1)}, u32[]{:S(2)}, u32[]{:S(2)}) %all-to-all-start) | async-done | bytes 1706016 | tf_op jit(solution)/shard_map/all_to_all | solution.py:16
  106.9 10.5 %reshape.39 = bf16[16,1,53312]{2,1,0:T(2,128)(2,1)S(1)} reshape(bf16[16,2,26656]{2,1,0:T(2,128)(2,1)} %all-to-all-done) | data formatting | bytes 3411968
  117.4 0.0 copy-start.5
  117.4 5.2 %convert_reduce_fusion = f32[53312]{0:T(1024)} fusion(bf16[16,1,53312]{2,1,0:T(2,128)(2,1)S(1)} %reshape.39), kind=kLoop, calls=%fused_computation | loop fusion | flops 1652672 | bytes 1919232 | tf_op jit(solution)/shard_map/reduce_sum | solution.py:23
  122.6 0.0 copy-start.3
  122.6 1.8 reshape.22
  124.5 0.0 all-reduce.8.cloned.1.call-update
  124.5 0.0 all-reduce.6.cloned.1.call-start
  124.5 0.0 copy-done.5
  124.5 1.7 convolution_reduce_fusion
  126.2 0.0 copy-start.2
  126.3 2.1 convolution_bitcast_fusion.1
  128.3 24.0 %all-reduce.8.cloned.1.call-done = f32[2,26656]{1,0:T(2,128)} async-done(((f32[2,26656]{1,0:T(2,128)}), f32[2,26656]{1,0:T(2,128)}) %all-reduce.8.cloned.1.call-update) | async-done | bytes 213264
  152.3 2.0 fusion
  154.3 0.1 reshape.27
  154.4 0.0 copy-done.3
  154.4 1.1 convolution_bitcast_fusion
  155.5 39.4 %all-reduce.2 = (f32[6]{0:T(128)S(1)}, f32[6]{0:T(128)S(1)}) all-reduce(f32[6]{0:T(128)S(1)} %convolution_bitcast_fusion, f32[6]{0:T(128)S(1)} %convolution_bitcast_fusion.1), channel_id=1, replica_groups=mesh['replica'=16,'spatial'=2] {'replica','spatial'}, use_global_device_ids=true, to_apply=%region_3.0 | all-reduce | flops 12 | bytes 96 | tf_op jit(solution)/shard_map/psum | solution.py:30
  194.9 0.8 convolution_reduce_fusion.1
  195.8 0.0 copy-done.2
  195.8 0.7 fusion.22
  196.5 0.1 broadcast.25
  196.6 0.6 dynamic-update-slice
  197.2 0.0 copy-start
  197.2 1.2 copy-done
  198.4 0.0 all-reduce.6.cloned.1.call-update
  198.4 133.0 %all-reduce.6.cloned.1.call-done = bf16[852992]{0:T(1024)(128)(2,1)} async-done(((bf16[852992]{0:T(1024)(128)(2,1)}), bf16[852992]{0:T(1024)(128)(2,1)}) %all-reduce.6.cloned.1.call-update) | async-done | bytes 1706000
  331.5 2.7 copy.13
  (3 shorter events, 0.0 us)
Async XLA Ops:
  65.0 7.7 %copy-start.1 = (f32[26656]{0:T(1024)S(1)}, f32[26656]{0:T(1024)}, u32[]{:S(2)}) copy-start(f32[26656]{0:T(1024)} %param.7) | copy-start | bytes 319876
  65.0 8.4 %copy-start.4 = (s32[6]{0:T(128)S(1)}, s32[6]{0:T(128)}, u32[]{:S(2)}) copy-start(s32[6]{0:T(128)} %param.10) | copy-start | bytes 76
  65.0 8.4 %copy-start.6 = (s32[6]{0:T(128)S(1)}, s32[6]{0:T(128)}, u32[]{:S(2)}) copy-start(s32[6]{0:T(128)} %param.9) | copy-start | bytes 76
  65.0 8.4 %copy-start.7 = (u32[32]{0:T(128)S(1)}, u32[32]{0:T(128)}, u32[]{:S(2)}) copy-start(u32[32]{0:T(128)} %constant.36) | copy-start | bytes 388
  65.0 41.9 %all-to-all-start = ((bf16[16,2,26656]{2,1,0:T(2,128)(2,1)}), bf16[16,2,26656]{2,1,0:T(2,128)(2,1)}, u32[]{:S(2)}, u32[]{:S(2)}) async-start(bf16[16,2,26656]{2,1,0:T(2,128)(2,1)} %reshape.38), calls=%async_computation | async-start | bytes 3424256 | tf_op jit(solution)/shard_map/all_to_all | solution.py:16
  72.5 79.8 %all-reduce.8.cloned.1.call-start = ((), (), s32[]{:S(2)}) async-start(), calls=%async_computation.2 | async-start | bytes 428032
  117.4 7.1 %copy-start.5 = (s32[6]{0:T(128)S(1)}, s32[6]{0:T(128)}, u32[]{:S(2)}) copy-start(s32[6]{0:T(128)} %param.11) | copy-start | bytes 76
  122.6 31.8 %copy-start.3 = (s32[26656]{0:T(1024)S(1)}, s32[26656]{0:T(1024)}, u32[]{:S(2)}) copy-start(s32[26656]{0:T(1024)} %iota_add_fusion) | copy-start | bytes 319876
  124.5 207.0 %all-reduce.6.cloned.1.call-start = ((), (), s32[]{:S(2)}) async-start(), calls=%async_computation.1 | async-start | bytes 3411968
  126.2 69.5 %copy-start.2 = (f32[26656]{0:T(1024)S(1)}, f32[26656]{0:T(1024)}, u32[]{:S(2)}) copy-start(f32[26656]{0:T(1024)} %param.8) | copy-start | bytes 319876
  197.2 1.2 copy-start
Sparse Core Ops, SparseCore 0:
  124.6 27.6 all-reduce.7
  198.6 132.8 all-reduce.5
where the time goes:
time: 342 us; the launch traced here: 341 us
  waiting for transfers between devices  189 us (55%)
  other arithmetic  59.7 us (17%)
  blocking collectives  39.4 us (12%)
  local copies, waits for them, and re-layouts  25.2 us (7%)
  between operations  14.2 us (4%)
  starting transfers between devices  7.66 us (2%)
  matrix products  5.68 us (2%)
    unnamed x4, waiting for transfers between devices  157 us
    psum x1, blocking collectives, shards(): wsq, gsq = lax.psum((wsq_local, gsq_local), ('replica', 'spatial'))  39.4 us
    unnamed x1, other arithmetic  37.8 us
    all_to_all x1, waiting for transfers between devices, shards(): lax.all_to_all(grads[0, 0].reshape(n_rep, n_spa * shard), 'replica', spli...  32.2 us
    unnamed x22, local copies, waits for them, and re-layouts  19.1 us
    all_to_all x1, other arithmetic, shards(): lax.all_to_all(grads[0, 0].reshape(n_rep, n_spa * shard), 'replica', spli...  13.3 us
    all_to_all x1, starting transfers between devices, shards(): lax.all_to_all(grads[0, 0].reshape(n_rep, n_spa * shard), 'replica', spli...  7.57 us
  transfers between devices with their start and end apart: 3, of which 3 were waited for; matrix products, arithmetic and copies ran while one was open for 2% of the time, Pallas kernels for 0%

commit v1 on v0

--- a/solution.py
+++ b/solution.py
@@ -2,6 +2,7 @@
 import jax.numpy as jnp
 from jax import lax
 from jax.sharding import PartitionSpec as P
+from jax.lax import psum
 
 
 def shards(grads, master, velocity, layer_offsets, layer_sizes, lars_skip):
@@ -27,7 +28,7 @@
     grad = summed.reshape(shard) / (n_rep * n_spa)
     gsq_local = jnp.dot(onehot, grad * grad, precision=lax.Precision.HIGHEST)
     wsq_local = jnp.dot(onehot, master * master, precision=lax.Precision.HIGHEST)
-    wsq, gsq = lax.psum((wsq_local, gsq_local), ("replica", "spatial"))
+    wsq, gsq = psum(psum((wsq_local, gsq_local), axis_name="replica"), axis_name="spatial")
     wnorm = jnp.sqrt(wsq)
     gnorm = jnp.sqrt(gsq)
     skipped = lars_skip.astype(jnp.float32)

time: 342 us -> 336 us (0.982)
  waiting for transfers between devices: 189 us -> 185 us
    unnamed x4, waiting for transfers between devices: 157 us -> 153 us
    psum x1 -> x2, blocking collectives: 39.4 us -> 37.8 us  [the longest x1 32.8 us: shards(): psum((wsq_local, gsq_local), axis_name='replica')]
where the time goes in v1:
time: 336 us; the launch traced here: 335 us
  waiting for transfers between devices  185 us (55%)
  other arithmetic  59.7 us (18%)
  blocking collectives  37.8 us (11%)
  local copies, waits for them, and re-layouts  25.2 us (8%)
  between operations  14.2 us (4%)
  starting transfers between devices  7.66 us (2%)
  matrix products  5.68 us (2%)
    unnamed x4, waiting for transfers between devices  153 us
    unnamed x1, other arithmetic  37.8 us
    psum x1, blocking collectives, shards(): psum((wsq_local, gsq_local), axis_name='replica')  32.8 us
    all_to_all x1, waiting for transfers between devices, shards(): lax.all_to_all(grads[0, 0].reshape(n_rep, n_spa * shard), 'replica', spli...  32.2 us
    unnamed x22, local copies, waits for them, and re-layouts  19.1 us
    all_to_all x1, other arithmetic, shards(): lax.all_to_all(grads[0, 0].reshape(n_rep, n_spa * shard), 'replica', spli...  13.3 us
    all_to_all x1, starting transfers between devices, shards(): lax.all_to_all(grads[0, 0].reshape(n_rep, n_spa * shard), 'replica', spli...  7.57 us
  transfers between devices with their start and end apart: 3, of which 3 were waited for; matrix products, arithmetic and copies ran while one was open for 2% of the time, Pallas kernels for 0%

profile of v1, /device:TPU:0, one launch (start us, length us, event | category | flops | bytes accessed | tf_op | source)
XLA Modules:
  0.0 335.2 jit_solution(15092341883991221009)
XLA Ops:
  7.2 37.8 %reduce.1 = bf16[852992]{0:T(1024)(128)(2,1)} reduce(bf16[1,1,852992]{2,1,0:T(2,128)(2,1)} %param.6, bf16[]{:T(256)} %constant.38), dimensions={0,1}, to_apply=%param.6.reduce_sub_computation | reduce | bytes 3411970 | tf_op args[0]
  44.9 3.0 all_to_all.8
  47.9 0.5 broadcast.54
  48.4 13.3 %reduce.8 = bf16[16,53312]{1,0:T(8,128)(2,1)} reduce(bf16[16,1,53312]{2,1,0:T(2,128)(2,1)S(1)} %all_to_all.8, bf16[]{:T(256)} %broadcast.54), dimensions={1}, to_apply=%all_to_all.8.reduce_sub_computation | reduce | bytes 3411970 | tf_op jit(solution)/shard_map/all_to_all | solution.py:17
  61.8 3.2 reshape.38
  65.0 0.0 copy-start.1
  65.0 0.0 copy-start.4
  65.0 0.0 copy-start.6
  65.0 0.0 copy-start.7
  65.0 7.6 %all-to-all-start = ((bf16[16,2,26656]{2,1,0:T(2,128)(2,1)}), bf16[16,2,26656]{2,1,0:T(2,128)(2,1)}, u32[]{:S(2)}, u32[]{:S(2)}) async-start(bf16[16,2,26656]{2,1,0:T(2,128)(2,1)} %reshape.38), calls=%async_computation | async-start | bytes 3424256 | tf_op jit(solution)/shard_map/all_to_all | solution.py:17
  72.5 0.0 all-reduce.9.cloned.1.call-start
  72.6 0.0 copy-done.1
  72.6 0.7 reshape.25
  73.4 0.0 copy-done.4
  73.4 0.0 copy-done.6
  73.4 0.0 copy-done.7
  73.4 0.7 dynamic-slice
  74.1 0.7 iota_add_fusion
  74.7 32.2 %all-to-all-done = bf16[16,2,26656]{2,1,0:T(2,128)(2,1)} async-done(((bf16[16,2,26656]{2,1,0:T(2,128)(2,1)}), bf16[16,2,26656]{2,1,0:T(2,128)(2,1)}, u32[]{:S(2)}, u32[]{:S(2)}) %all-to-all-start) | async-done | bytes 1706016 | tf_op jit(solution)/shard_map/all_to_all | solution.py:17
  106.9 10.5 %reshape.39 = bf16[16,1,53312]{2,1,0:T(2,128)(2,1)S(1)} reshape(bf16[16,2,26656]{2,1,0:T(2,128)(2,1)} %all-to-all-done) | data formatting | bytes 3411968
  117.4 0.0 copy-start.5
  117.4 5.2 %convert_reduce_fusion = f32[53312]{0:T(1024)} fusion(bf16[16,1,53312]{2,1,0:T(2,128)(2,1)S(1)} %reshape.39), kind=kLoop, calls=%fused_computation | loop fusion | flops 1652672 | bytes 1919232 | tf_op jit(solution)/shard_map/reduce_sum | solution.py:24
  122.6 0.0 copy-start.3
  122.6 1.8 reshape.22
  124.5 0.0 all-reduce.9.cloned.1.call-update
  124.5 0.0 all-reduce.7.cloned.1.call-start
  124.5 0.0 copy-done.5
  124.5 1.7 convolution_reduce_fusion
  126.2 0.0 copy-start.2
  126.3 2.1 convolution_bitcast_fusion.1
  128.3 24.0 %all-reduce.9.cloned.1.call-done = f32[2,26656]{1,0:T(2,128)} async-done(((f32[2,26656]{1,0:T(2,128)}), f32[2,26656]{1,0:T(2,128)}) %all-reduce.9.cloned.1.call-update) | async-done | bytes 213264
  152.3 2.0 fusion
  154.3 0.1 reshape.27
  154.4 0.0 copy-done.3
  154.4 1.1 convolution_bitcast_fusion
  155.5 32.8 %all-reduce.2 = (f32[6]{0:T(128)S(1)}, f32[6]{0:T(128)S(1)}) all-reduce(f32[6]{0:T(128)S(1)} %convolution_bitcast_fusion, f32[6]{0:T(128)S(1)} %convolution_bitcast_fusion.1), channel_id=1, replica_groups=mesh['replica'=16,'spatial'=2] {'replica'}, use_global_device_ids=true, to_apply=%region_4.0 | all-reduce | flops 12 | bytes 96 | tf_op jit(solution)/shard_map/psum | solution.py:31
  188.4 4.9 %all-reduce.3 = (f32[6]{0:T(128)S(1)}, f32[6]{0:T(128)S(1)}) all-reduce(f32[6]{0:T(128)S(1)} %get-tuple-element.3, f32[6]{0:T(128)S(1)} %get-tuple-element.4), channel_id=1, replica_groups=mesh['replica'=16,'spatial'=2] {'spatial'}, use_global_device_ids=true, to_apply=%region_5.0 | all-reduce | flops 12 | bytes 96 | tf_op jit(solution)/shard_map/psum | solution.py:31
  193.3 0.8 convolution_reduce_fusion.1
  194.1 0.0 copy-done.2
  194.1 0.7 fusion.22
  194.8 0.1 broadcast.25
  194.9 0.6 dynamic-update-slice
  195.6 0.0 copy-start
  195.6 1.2 copy-done
  196.7 0.0 all-reduce.7.cloned.1.call-update
  196.8 128.8 %all-reduce.7.cloned.1.call-done = bf16[852992]{0:T(1024)(128)(2,1)} async-done(((bf16[852992]{0:T(1024)(128)(2,1)}), bf16[852992]{0:T(1024)(128)(2,1)}) %all-reduce.7.cloned.1.call-update) | async-done | bytes 1706000
  325.6 2.7 copy.13
  (3 shorter events, 0.0 us)
Async XLA Ops:
  65.0 7.7 %copy-start.1 = (f32[26656]{0:T(1024)S(1)}, f32[26656]{0:T(1024)}, u32[]{:S(2)}) copy-start(f32[26656]{0:T(1024)} %param.7) | copy-start | bytes 319876
  65.0 8.4 %copy-start.4 = (s32[6]{0:T(128)S(1)}, s32[6]{0:T(128)}, u32[]{:S(2)}) copy-start(s32[6]{0:T(128)} %param.10) | copy-start | bytes 76
  65.0 8.4 %copy-start.6 = (s32[6]{0:T(128)S(1)}, s32[6]{0:T(128)}, u32[]{:S(2)}) copy-start(s32[6]{0:T(128)} %param.9) | copy-start | bytes 76
  65.0 8.4 %copy-start.7 = (u32[32]{0:T(128)S(1)}, u32[32]{0:T(128)}, u32[]{:S(2)}) copy-start(u32[32]{0:T(128)} %constant.36) | copy-start | bytes 388
  65.0 41.9 %all-to-all-start = ((bf16[16,2,26656]{2,1,0:T(2,128)(2,1)}), bf16[16,2,26656]{2,1,0:T(2,128)(2,1)}, u32[]{:S(2)}, u32[]{:S(2)}) async-start(bf16[16,2,26656]{2,1,0:T(2,128)(2,1)} %reshape.38), calls=%async_computation | async-start | bytes 3424256 | tf_op jit(solution)/shard_map/all_to_all | solution.py:17
  72.5 79.8 %all-reduce.9.cloned.1.call-start = ((), (), s32[]{:S(2)}) async-start(), calls=%async_computation.2 | async-start | bytes 428032
  117.4 7.1 %copy-start.5 = (s32[6]{0:T(128)S(1)}, s32[6]{0:T(128)}, u32[]{:S(2)}) copy-start(s32[6]{0:T(128)} %param.11) | copy-start | bytes 76
  122.6 31.8 %copy-start.3 = (s32[26656]{0:T(1024)S(1)}, s32[26656]{0:T(1024)}, u32[]{:S(2)}) copy-start(s32[26656]{0:T(1024)} %iota_add_fusion) | copy-start | bytes 319876
  124.5 201.1 %all-reduce.7.cloned.1.call-start = ((), (), s32[]{:S(2)}) async-start(), calls=%async_computation.1 | async-start | bytes 3411968
  126.2 67.8 %copy-start.2 = (f32[26656]{0:T(1024)S(1)}, f32[26656]{0:T(1024)}, u32[]{:S(2)}) copy-start(f32[26656]{0:T(1024)} %param.8) | copy-start | bytes 319876
  195.6 1.2 copy-start
Sparse Core Ops, SparseCore 0:
  124.6 27.6 all-reduce.8
  196.9 128.6 all-reduce.6
